TPU v7x, 128 devices: a whole 4x4x4 slice. The times are simulated.
128 devices in a mesh: lon: 16 (over y_hi, z, core), mem: 8 (over x, y_lo).
Axes of the slice: x: 4, y: 4 (y_hi: 2, y_lo: 2; y = y_hi * 2 + y_lo), z: 4, core: 2. Of those that a mesh axis runs over, the one named last changes fastest.
Arguments:
- alpha: bfloat16 [80, 128, 512, 128], P('mem', 'lon'), may hold values from -6 to 6
- ens_pert: bfloat16 [80, 128, 512, 128], P('mem', None, 'lon'), may hold values from -6 to 6
- vert_sqrt: bfloat16 [128, 128], replicated, may hold values from -0.5 to 0.5
- lat_sqrt: bfloat16 [128, 128], replicated, may hold values from -0.5 to 0.5
Outputs:
- increment: float32 [128, 512, 128], P('mem', 'lon')
All inputs are finite; a program needn't handle non-finite values.
Results may differ from a plain program's by a relative error of at most 0.0042.
Values may be sent and summed in bfloat16 or wider, within the bound.
A program may use at most 128 MiB of HBM per device.

v0:
```python
import math

import jax
import jax.numpy as jnp
from jax import lax
from jax.sharding import PartitionSpec as P


def in_blocks(value, dim, size):
    before, after = (value.shape[:dim], value.shape[dim + 1 :])
    return jnp.moveaxis(value.reshape(*before, size, -1, *after), dim, 0)


def sent_and_summed(value, axis, dim):
    size = lax.axis_size(axis)
    parts = lax.all_to_all(in_blocks(value, dim, size), axis, 0, 0, tiled=True)
    return jnp.sum(parts.astype(jnp.float32), axis=0)


def localize(fields, vert_sqrt, lat_sqrt):
    vertical = jnp.einsum(
        "kl,mlxi->mkxi", vert_sqrt, fields, preferred_element_type=jnp.float32
    ).astype(jnp.bfloat16)
    stacked = jnp.dot(
        vertical.reshape(-1, fields.shape[3]), lat_sqrt, preferred_element_type=jnp.float32
    )
    return stacked.reshape(fields.shape[0], vert_sqrt.shape[0], fields.shape[2], lat_sqrt.shape[1])


def local(alpha, ens_pert, vert_sqrt, lat_sqrt):
    members_all = ens_pert.shape[0] * lax.axis_size("mem")
    factor = 1.0 / math.sqrt(members_all)
    columns = lax.all_to_all(alpha, "lon", split_axis=2, concat_axis=1, tiled=True)
    localized = localize(columns, vert_sqrt, lat_sqrt)
    partial_value = jnp.sum(ens_pert.astype(jnp.float32) * localized, axis=0) * factor
    increment = sent_and_summed(partial_value.astype(jnp.bfloat16), "mem", 0)
    return increment


def solution(mesh):
    placed = (P("mem", "lon", None, None), P("mem", None, "lon", None), P(), P())
    return jax.shard_map(
        local, mesh=mesh, in_specs=placed, out_specs=P("mem", "lon", None), check_vma=False
    )
```

profile of v0, /device:TPU:1, one launch (start us, length us, event | category | flops | bytes accessed | tf_op | source)
XLA Modules:
  0.0 186.9 jit_solution(16066377604243369738)
XLA Ops:
  0.0 0.0 copy-start
  0.0 14.6 %copy.18 = bf16[10,8,512,128]{3,1,0,2:T(8,128)(2,1)} copy(bf16[10,8,512,128]{3,2,1,0:T(8,128)(2,1)} %param.4) | data formatting | bytes 20971520 | tf_op args[0]
  14.6 127.4 %all_to_all.23 = bf16[10,8,512,128]{3,1,0,2:T(8,128)(2,1)} all-to-all(bf16[10,8,512,128]{3,1,0,2:T(8,128)(2,1)} %copy.18), channel_id=1, replica_groups=mesh['lon'=16,'mem'=8] {'lon'}, dimensions={2} | all-to-all | bytes 20971520 | tf_op jit(solution)/shard_map/all_to_all | solution.py:33
  142.0 0.0 copy-start.1
  142.0 11.9 %copy.20 = bf16[10,16,8,32,128]{4,3,2,1,0:T(8,128)(2,1)} copy(bf16[10,16,8,32,128]{4,2,0,3,1:T(8,128)(2,1)} %bitcast.21) | data formatting | bytes 20971520 | tf_op jit(solution)/shard_map/all_to_all | solution.py:33
  153.9 0.0 copy-done
  153.9 0.0 copy-done.1
  153.9 13.8 %multiply_reduce_fusion = f32[128,32,128]{2,0,1:T(8,128)S(1)} fusion(bf16[10,128,32,128]{3,2,1,0:T(8,128)(2,1)} %param.5, bf16[10,128,32,128]{3,2,1,0:T(8,128)(2,1)} %bitcast.22, bf16[128,128]{1,0:T(8,128)(2,1)S(1)} %copy-done, bf16[128,128]{1,0:T(8,128)(2,1)S(1)} %copy-done.1), kind=kOutput, calls=%fused_computation | convolution fusion | flops 2704801792 | bytes 23134208 | tf_op jit(solution)/shard_map/dot_general | solution.py:24
  167.7 0.3 multiply_convert_fusion
  168.0 0.2 copy.23
  168.2 17.8 %all_to_all.24 = bf16[8,16,32,128]{3,1,2,0:T(8,128)(2,1)S(1)} all-to-all(bf16[8,16,32,128]{3,1,2,0:T(8,128)(2,1)S(1)} %copy.23), channel_id=1, replica_groups=mesh['lon'=16,'mem'=8] {'mem'}, dimensions={0} | all-to-all | bytes 2097152 | tf_op jit(solution)/shard_map/all_to_all | solution.py:16
  186.0 0.1 convert_reduce_fusion
  186.1 0.8 copy.25
Async XLA Ops:
  0.0 153.9 %copy-start = (bf16[128,128]{1,0:T(8,128)(2,1)S(1)}, bf16[128,128]{1,0:T(8,128)(2,1)}, u32[]{:S(2)}) copy-start(bf16[128,128]{1,0:T(8,128)(2,1)} %param.7) | copy-start | bytes 98308
  142.0 11.9 %copy-start.1 = (bf16[128,128]{1,0:T(8,128)(2,1)S(1)}, bf16[128,128]{1,0:T(8,128)(2,1)}, u32[]{:S(2)}) copy-start(bf16[128,128]{1,0:T(8,128)(2,1)} %param.6) | copy-start | bytes 98308
where the time goes:
time: 188 us; the launch traced here: 187 us
  blocking collectives  145 us (77%)
  local copies, waits for them, and re-layouts  27.4 us (15%)
  matrix products  13.8 us (7%)
    all_to_all x1, blocking collectives, local(): lax.all_to_all(alpha, 'lon', split_axis=2, concat_axis=1, tiled=True)  127 us
    all_to_all x1, blocking collectives, sent_and_summed(): parts = lax.all_to_all(in_blocks(value, dim, size), axis, 0, 0, tiled=True)  17.8 us
    unnamed x5, local copies, waits for them, and re-layouts  14.6 us
    dot_general x1, matrix products, localize(): jnp.dot(vertical.reshape(-1, fields.shape[3]), lat_sqrt, preferred_elemen...  13.8 us
    all_to_all x1, local copies, waits for them, and re-layouts, local(): lax.all_to_all(alpha, 'lon', split_axis=2, concat_axis=1, tiled=True)  11.9 us

commit v1 on v0

v1 whole, which is shorter than its diff:
```python
import functools
import math

import jax
import jax.numpy as jnp
from jax import lax
from jax.experimental import pallas as pl
from jax.experimental.pallas import tpu as pltpu
from jax.sharding import PartitionSpec as P

MESH = pl.DeviceIdType.MESH
ROWS = 8
PAIR = 2
WINDOW = 20


def kernel(
    factor, n_lon, n_mem, alpha_ref, pert_ref, vert_ref, lat_ref, out_ref,
    columns, perts, kron, lat_two, total, parts, arrived,
    own_sem, pert_sem, send_sem, recv_sem, part_send_sem, part_recv_sem,
):
    lon, mem = lax.axis_index("lon"), lax.axis_index("mem")
    members, levels_own = alpha_ref.shape[0], alpha_ref.shape[1]
    levels = levels_own * n_lon
    own_rows = pert_ref.shape[2]
    width = lat_ref.shape[0]
    chunks, pairs = own_rows // ROWS, members // PAIR
    units = chunks * pairs
    stacked = levels * ROWS
    levels_out = levels // n_mem

    def lon_peer(dy, dz, dc):
        y, z, c = lon // 8, (lon // 2) % 4, lon % 2
        return ((y + dy) % 2) * 8 + ((z + dz) % 4) * 2 + (c + dc) % 2

    lon_peers = [
        lon_peer(dy, dz, dc)
        for dz in (2, 1, 3, 0) for dy in (1, 0) for dc in (0, 1)
        if (dy, dz, dc) != (0, 0, 0)
    ]
    mem_peers = [(mem + step) % n_mem for step in range(1, n_mem)]

    barrier = pltpu.get_barrier_semaphore()
    for peer in lon_peers:
        pl.semaphore_signal(barrier, inc=1, device_id={"lon": peer, "mem": mem}, device_id_type=MESH)
    for peer in mem_peers:
        pl.semaphore_signal(barrier, inc=1, device_id={"lon": lon, "mem": peer}, device_id_type=MESH)

    def own_copy(chunk):
        rows = pl.ds(pl.multiple_of(lon * own_rows + chunk * ROWS, ROWS), ROWS)
        return pltpu.make_async_copy(
            alpha_ref.at[:, :, rows, :],
            columns.at[chunk, :, pl.ds(lon * levels_own, levels_own)],
            own_sem.at[chunk],
        )

    def pert_copy(chunk):
        rows = pl.ds(pl.multiple_of(chunk * ROWS, ROWS), ROWS)
        return pltpu.make_async_copy(pert_ref.at[:, :, rows, :], perts.at[chunk], pert_sem.at[chunk])

    def send(unit):
        chunk, pair = unit // pairs, unit % pairs
        group = pl.ds(pair * PAIR, PAIR)
        for peer in lon_peers:
            rows = pl.ds(pl.multiple_of(peer * own_rows + chunk * ROWS, ROWS), ROWS)
            pltpu.make_async_remote_copy(
                src_ref=alpha_ref.at[group, :, rows, :],
                dst_ref=columns.at[chunk, group, pl.ds(lon * levels_own, levels_own)],
                send_sem=send_sem, recv_sem=recv_sem.at[unit],
                device_id={"lon": peer, "mem": mem}, device_id_type=MESH,
            ).start()

    pl.semaphore_wait(barrier, len(lon_peers) + len(mem_peers))

    def first_sends(unit, carry):
        send(unit)
        return carry

    lax.fori_loop(0, min(WINDOW, units), first_sends, 0)
    for chunk in range(chunks):
        own_copy(chunk).start()
        pert_copy(chunk).start()

    wide = (levels, stacked)
    spread = (
        lax.broadcasted_iota(jnp.int32, wide, 1) // ROWS == lax.broadcasted_iota(jnp.int32, wide, 0)
    ).astype(jnp.bfloat16)
    band = (
        lax.broadcasted_iota(jnp.int32, (levels, levels // ROWS), 0) // ROWS
        == lax.broadcasted_iota(jnp.int32, (levels, levels // ROWS), 1)
    ).astype(jnp.bfloat16)

    same = lax.broadcasted_iota(jnp.int32, wide, 0) % ROWS == lax.broadcasted_iota(jnp.int32, wide, 1) % ROWS

    def build(block, carry):
        tall = levels // ROWS
        some = vert_ref[pl.ds(pl.multiple_of(block * tall, tall), tall), :]
        tallest = jnp.dot(band, some, preferred_element_type=jnp.float32).astype(jnp.bfloat16)
        full = jnp.dot(tallest, spread, preferred_element_type=jnp.float32)
        kron[pl.ds(pl.multiple_of(block * levels, levels), levels), :] = jnp.where(same, full, 0.0).astype(jnp.bfloat16)
        return carry

    lax.fori_loop(0, stacked // levels, build, 0)
    lat_two[...] = jnp.zeros_like(lat_two)
    lat_two[pl.ds(0, width), pl.ds(0, width)] = lat_ref[...]
    lat_two[pl.ds(width, width), pl.ds(width, width)] = lat_ref[...]

    def part_copy(chunk, peer):
        return pltpu.make_async_remote_copy(
            src_ref=parts.at[chunk, pl.ds(peer * levels_out, levels_out)],
            dst_ref=arrived.at[chunk, mem],
            send_sem=part_send_sem, recv_sem=part_recv_sem.at[chunk],
            device_id={"lon": lon, "mem": peer}, device_id_type=MESH,
        )

    def finish(chunk):
        others = arrived.at[chunk, pl.ds(0, n_mem - 1)]
        pltpu.make_async_copy(others, others, part_recv_sem.at[chunk]).wait()
        value = arrived[chunk, 0].astype(jnp.float32)
        for source in range(1, n_mem):
            value = value + arrived[chunk, source].astype(jnp.float32)
        out_ref[:, pl.ds(pl.multiple_of(chunk * ROWS, ROWS), ROWS), :] = value

    def chunk_step(chunk, carry):
        own_copy(chunk).wait()
        pert_copy(chunk).wait()
        total[...] = jnp.zeros_like(total)

        def unit_step(pair, carry):
            unit = chunk * pairs + pair
            if WINDOW < units:
                @pl.when(unit + WINDOW < units)
                def _():
                    send(unit + WINDOW)
            landed = columns.at[chunk, pl.ds(pair * PAIR, PAIR), pl.ds(0, levels - levels_own)]
            pltpu.make_async_copy(landed, landed, recv_sem.at[unit]).wait()
            both = jnp.concatenate(
                [columns[chunk, pair * PAIR + k].reshape(stacked, width) for k in range(PAIR)], axis=1
            )
            vertical = jnp.dot(kron[...], both, preferred_element_type=jnp.float32).astype(jnp.bfloat16)
            localized = jnp.dot(vertical, lat_two[...], preferred_element_type=jnp.float32)
            value = total[...]
            for k in range(PAIR):
                pert = perts[chunk, pair * PAIR + k].reshape(stacked, width).astype(jnp.float32)
                value = value + pert * localized[:, k * width : (k + 1) * width]
            total[...] = value
            return carry

        lax.fori_loop(0, pairs, unit_step, 0)
        parts[chunk] = (total[...] * factor).astype(jnp.bfloat16).reshape(levels, ROWS, width)
        for peer in mem_peers:
            part_copy(chunk, peer).start()
        arrived[chunk, mem] = parts[chunk, pl.ds(mem * levels_out, levels_out)]

        @pl.when(chunk > 0)
        def _():
            finish(chunk - 1)

        return carry

    lax.fori_loop(0, chunks, chunk_step, 0)
    finish(chunks - 1)

    sent = columns.at[:, :, pl.ds(0, levels - levels_own)]
    pltpu.make_async_copy(sent, sent, send_sem).wait()
    sent = arrived.at[:, pl.ds(0, n_mem - 1)]
    pltpu.make_async_copy(sent, sent, part_send_sem).wait()


def local(alpha, ens_pert, vert_sqrt, lat_sqrt):
    n_lon, n_mem = lax.axis_size("lon"), lax.axis_size("mem")
    members, levels_own, _, width = alpha.shape
    _, levels, own_rows, _ = ens_pert.shape
    chunks = own_rows // ROWS
    units = chunks * (members // PAIR)
    stacked = levels * ROWS
    levels_out = levels // n_mem
    factor = 1.0 / math.sqrt(members * n_mem)
    vmem = pl.BlockSpec(memory_space=pltpu.VMEM)
    hbm = pl.BlockSpec(memory_space=pl.ANY)
    return pl.pallas_call(
        functools.partial(kernel, factor, n_lon, n_mem),
        out_shape=jax.ShapeDtypeStruct((levels_out, own_rows, width), jnp.float32),
        in_specs=[hbm, hbm, vmem, vmem],
        out_specs=vmem,
        scratch_shapes=[
            pltpu.VMEM((chunks, members, levels, ROWS, width), jnp.bfloat16),
            pltpu.VMEM((chunks, members, levels, ROWS, width), jnp.bfloat16),
            pltpu.VMEM((stacked, stacked), jnp.bfloat16),
            pltpu.VMEM((PAIR * width, PAIR * width), jnp.bfloat16),
            pltpu.VMEM((stacked, width), jnp.float32),
            pltpu.VMEM((chunks, levels, ROWS, width), jnp.bfloat16),
            pltpu.VMEM((chunks, n_mem, levels_out, ROWS, width), jnp.bfloat16),
            pltpu.SemaphoreType.DMA((chunks,)),
            pltpu.SemaphoreType.DMA((chunks,)),
            pltpu.SemaphoreType.DMA,
            pltpu.SemaphoreType.DMA((units,)),
            pltpu.SemaphoreType.DMA,
            pltpu.SemaphoreType.DMA((chunks,)),
        ],
        compiler_params=pltpu.CompilerParams(
            collective_id=0, has_side_effects=True, vmem_limit_bytes=60 * 2**20
        ),
    )(alpha, ens_pert, vert_sqrt, lat_sqrt)


def solution(mesh):
    placed = (P("mem", "lon", None, None), P("mem", None, "lon", None), P(), P())
    return jax.shard_map(
        local, mesh=mesh, in_specs=placed, out_specs=P("mem", "lon", None), check_vma=False
    )
```

time: 188 us -> 147 us (0.78)
  blocking collectives: 145 us -> 0 us
  Pallas kernels: 0 us -> 144 us
  local copies, waits for them, and re-layouts: 27.4 us -> 1.67 us
  matrix products: 13.8 us -> 0 us
    all_to_all x2 -> x0, blocking collectives: 145 us -> none  [the longest x1 127 us: local(): lax.all_to_all(alpha, 'lon', split_axis=2, concat_axis=1, tiled=True)]
    pallas_call x0 -> x1, Pallas kernels: none -> 144 us  [local(): pl.pallas_call(functools.partial(kernel, factor, n_lon, n_mem), out_shape...]
    dot_general x1 -> x0, matrix products: 13.8 us -> none  [localize(): jnp.dot(vertical.reshape(-1, fields.shape[3]), lat_sqrt, preferred_elemen...]
    unnamed x5 -> x1, local copies, waits for them, and re-layouts: 14.6 us -> 1.67 us
    all_to_all x1 -> x0, local copies, waits for them, and re-layouts: 11.9 us -> none  [local(): lax.all_to_all(alpha, 'lon', split_axis=2, concat_axis=1, tiled=True)]
where the time goes in v1:
time: 147 us; the launch traced here: 146 us
  Pallas kernels  144 us (98%)
  local copies, waits for them, and re-layouts  1.67 us (1%)
    pallas_call x1, Pallas kernels, local(): pl.pallas_call(functools.partial(kernel, factor, n_lon, n_mem), out_shape...  144 us

profile of v1, /device:TPU:1, one launch (start us, length us, event | category | flops | bytes accessed | tf_op | source)
XLA Modules:
  0.0 145.7 jit_solution(10103780008262285075)
XLA Ops:
  0.0 144.0 %shard_map.46 = f32[16,32,128]{2,1,0:T(8,128)} custom-call(bf16[10,8,512,128]{3,2,1,0:T(8,128)(2,1)} %alpha_ref.1, bf16[10,128,32,128]{3,2,1,0:T(8,128)(2,1)} %pert_ref.1, bf16[128,128]{1,0:T(8,128)(2,1)} %vert_ref.1, bf16[128,128]{1,0:T(8,128)(2,1)} %lat_ref.1), custom_call_target="tpu_custom_call" | custom-call | tf_op jit(solution)/shard_map/pallas_call | solution.py:181
  144.1 1.7 %copy.6 = f32[16,32,128]{2,1,0:T(8,128)} copy(f32[16,32,128]{2,1,0:T(8,128)} %shard_map.46) | data formatting | bytes 524288

commit v2 on v1

v2 whole, which is shorter than its diff:
```python
import functools
import math

import jax
import jax.numpy as jnp
from jax import lax
from jax.experimental import pallas as pl
from jax.experimental.pallas import tpu as pltpu
from jax.sharding import PartitionSpec as P

MESH = pl.DeviceIdType.MESH
ROWS = 8
PAIR = 2
WINDOW = 15
LIMIT = 54
HALF = True
STAGGER = True


def kernel(
    factor, n_lon, n_mem, alpha_ref, pert_ref, vert_ref, lat_ref, out_ref,
    columns, perts, staged, vert, kron, lat_two, total, parts, runs, held, halves, second, arrived,
    stage_sem, small_sem, own_sem, pert_sem, send_sem, recv_sem,
    run_send, run_recv, half_send, half_recv, last_send, last_recv,
):
    lon, mem = lax.axis_index("lon"), lax.axis_index("mem")
    members, levels_own = alpha_ref.shape[0], alpha_ref.shape[1]
    levels = levels_own * n_lon
    own_rows = pert_ref.shape[2]
    width = lat_ref.shape[0]
    chunks, pairs = own_rows // ROWS, members // PAIR
    units = chunks * pairs
    stacked = levels * ROWS
    levels_out = levels // n_mem
    n_run = n_mem // 2
    mem_x, mem_y = mem // 2, mem % 2
    last = chunks - 1

    def lon_peer(dy, dz, dc):
        y, z, c = lon // 8, (lon // 2) % 4, lon % 2
        return ((y + dy) % 2) * 8 + ((z + dz) % 4) * 2 + (c + dc) % 2

    lon_peers = [
        lon_peer(dy, dz, dc)
        for dz in (2, 1, 3, 0) for dy in (1, 0) for dc in (0, 1)
        if (dy, dz, dc) != (0, 0, 0)
    ]
    mem_peers = [(mem + step) % n_mem for step in range(1, n_mem)]

    def wait_for(ref, sem):
        pltpu.make_async_copy(ref, ref, sem).wait()

    barrier = pltpu.get_barrier_semaphore()
    for peer in lon_peers:
        pl.semaphore_signal(barrier, inc=1, device_id={"lon": peer, "mem": mem}, device_id_type=MESH)
    for peer in mem_peers:
        pl.semaphore_signal(barrier, inc=1, device_id={"lon": lon, "mem": peer}, device_id_type=MESH)

    def own_copy(chunk):
        rows = pl.ds(pl.multiple_of(lon * own_rows + chunk * ROWS, ROWS), ROWS)
        return pltpu.make_async_copy(
            alpha_ref.at[:, :, rows, :],
            columns.at[chunk, :, pl.ds(lon * levels_own, levels_own)],
            own_sem.at[chunk],
        )

    def pert_copy(chunk):
        rows = pl.ds(pl.multiple_of(chunk * ROWS, ROWS), ROWS)
        return pltpu.make_async_copy(pert_ref.at[:, :, rows, :], perts.at[chunk], pert_sem.at[chunk])

    def send_to(peer, source, unit):
        chunk, pair = unit // pairs, unit % pairs
        group = pl.ds(pair * PAIR, PAIR)
        rows = pl.ds(pl.multiple_of(peer * own_rows + chunk * ROWS, ROWS), ROWS)
        pltpu.make_async_remote_copy(
            src_ref=source.at[group, :, rows, :],
            dst_ref=columns.at[chunk, group, pl.ds(lon * levels_own, levels_own)],
            send_sem=send_sem, recv_sem=recv_sem.at[unit],
            device_id={"lon": peer, "mem": mem}, device_id_type=MESH,
        ).start()

    def send(unit, carry):
        for peer in lon_peers:
            send_to(peer, alpha_ref, unit)
        return carry

    def send_late(step):
        core, pair = step // pairs, step % pairs
        unit = last * pairs + pair
        for dz in (2, 1, 3, 0):
            for dy in (1, 0):
                if (dy, dz) != (0, 0):
                    send_to(lon_peer(dy, dz, core + lon), alpha_ref, unit)

        @pl.when(lon % 2 != core)
        def _():
            send_to(lon_peer(0, 0, 1), alpha_ref, unit)

    def send_ahead(unit):
        early = last * pairs
        if not STAGGER:
            @pl.when(unit < units)
            def _():
                send(unit, 0)
            return

        @pl.when(unit < early)
        def _():
            send(unit, 0)

        @pl.when((unit >= early) & (unit < units))
        def _():
            for step in range(2):
                send_late((unit - early) * 2 + step)

    stage = pltpu.make_async_copy(alpha_ref.at[pl.ds(0, PAIR)], staged, stage_sem)
    stage.start()
    vert_copy = pltpu.make_async_copy(vert_ref, vert, small_sem.at[0])
    vert_copy.start()
    lat_two[...] = jnp.zeros_like(lat_two)
    stage.wait()
    pl.semaphore_wait(barrier, len(lon_peers) + len(mem_peers))

    for peer in lon_peers:
        send_to(peer, staged, 0)
    lax.fori_loop(1, min(WINDOW, units), send, 0)
    lat_copies = [
        pltpu.make_async_copy(
            lat_ref, lat_two.at[pl.ds(k * width, width), pl.ds(k * width, width)], small_sem.at[1 + k]
        )
        for k in range(PAIR)
    ]
    for copy in lat_copies:
        copy.start()
    for chunk in range(chunks):
        own_copy(chunk).start()
        pert_copy(chunk).start()

    wide = (levels, stacked)
    spread = (
        lax.broadcasted_iota(jnp.int32, wide, 1) // ROWS == lax.broadcasted_iota(jnp.int32, wide, 0)
    ).astype(jnp.bfloat16)
    tall = levels // ROWS
    band = (
        lax.broadcasted_iota(jnp.int32, (levels, tall), 0) // ROWS == lax.broadcasted_iota(jnp.int32, (levels, tall), 1)
    ).astype(jnp.bfloat16)
    same = lax.broadcasted_iota(jnp.int32, wide, 0) % ROWS == lax.broadcasted_iota(jnp.int32, wide, 1) % ROWS

    def build(block, carry):
        some = vert[pl.ds(pl.multiple_of(block * tall, tall), tall), :]
        repeated = jnp.dot(band, some, preferred_element_type=jnp.float32).astype(jnp.bfloat16)
        full = jnp.dot(repeated, spread, preferred_element_type=jnp.float32)
        kron[pl.ds(pl.multiple_of(block * levels, levels), levels), :] = jnp.where(same, full, 0.0).astype(jnp.bfloat16)
        return carry

    vert_copy.wait()
    lax.fori_loop(0, stacked // levels, build, 0)
    for copy in lat_copies:
        copy.wait()

    def to_device(src, dst, send_sem, recv_sem, peer):
        pltpu.make_async_remote_copy(
            src_ref=src, dst_ref=dst, send_sem=send_sem, recv_sem=recv_sem,
            device_id={"lon": lon, "mem": peer}, device_id_type=MESH,
        ).start()

    def start_runs(chunk):
        parts[chunk] = (total[...] * factor).astype(jnp.bfloat16).reshape(levels, ROWS, width)
        for step in (2, 1, 3):
            peer = (mem_x + step) % n_run
            to_device(
                parts.at[chunk, pl.ds(peer * 2 * levels_out, 2 * levels_out)],
                runs.at[chunk, mem_x], run_send, run_recv.at[chunk], peer * 2 + mem_y,
            )

    def start_half(chunk):
        wait_for(runs.at[chunk, pl.ds(0, n_run - 1)], run_recv.at[chunk])

        def summed(half):
            first = half * levels_out
            value = parts[chunk, pl.ds(mem_x * 2 * levels_out + first, levels_out)].astype(jnp.float32)
            for step in range(1, n_run):
                source = (mem_x + step) % n_run
                value = value + runs[chunk, source, pl.ds(first, levels_out)].astype(jnp.float32)
            return value

        halves[chunk] = summed(1 - mem_y).astype(jnp.bfloat16)
        held[chunk] = summed(mem_y)
        if HALF:
            to_device(halves.at[chunk], second.at[chunk], half_send, half_recv.at[chunk], mem_x * 2 + 1 - mem_y)

    def finish(chunk):
        if HALF:
            wait_for(second.at[chunk], half_recv.at[chunk])
        out_ref[:, pl.ds(chunk * ROWS, ROWS), :] = held[chunk] + second[chunk].astype(jnp.float32)

    def start_last(peer):
        to_device(
            parts.at[last, pl.ds(peer * levels_out, levels_out)], arrived.at[mem], last_send, last_recv, peer
        )

    def finish_last():
        wait_for(arrived.at[pl.ds(0, n_mem - 1)], last_recv)
        value = parts[last, pl.ds(mem * levels_out, levels_out)].astype(jnp.float32)
        for source in mem_peers:
            value = value + arrived[source].astype(jnp.float32)
        out_ref[:, pl.ds(last * ROWS, ROWS), :] = value

    def landed(chunk, pair):
        wait_for(
            columns.at[chunk, pl.ds(pair * PAIR, PAIR), pl.ds(0, levels - levels_own)],
            recv_sem.at[chunk * pairs + pair],
        )
        return jnp.concatenate(
            [columns[chunk, pair * PAIR + k].reshape(stacked, width) for k in range(PAIR)], axis=1
        )

    def added(value, chunk, pair, both, first_level, n_levels):
        rows = pl.ds(first_level * ROWS, n_levels * ROWS)
        vertical = jnp.dot(kron[rows, :], both, preferred_element_type=jnp.float32).astype(jnp.bfloat16)
        localized = jnp.dot(vertical, lat_two[...], preferred_element_type=jnp.float32)
        for k in range(PAIR):
            pert = perts[chunk, pair * PAIR + k, pl.ds(first_level, n_levels)]
            pert = pert.reshape(n_levels * ROWS, width).astype(jnp.float32)
            value = value + pert * localized[:, k * width : (k + 1) * width]
        return value

    def units_of(chunk, n_pairs):
        own_copy(chunk).wait()
        pert_copy(chunk).wait()
        total[...] = jnp.zeros_like(total)

        def unit_step(pair, carry):
            unit = chunk * pairs + pair

            send_ahead(unit + WINDOW)

            both = landed(chunk, pair)

            @pl.when((chunk > 0) & (pair == jnp.where(chunk < last, 1, 1 - lon % 2)))
            def _():
                start_half(chunk - 1)

            total[...] = added(total[...], chunk, pair, both, 0, levels)
            return carry

        lax.fori_loop(0, n_pairs, unit_step, 0)

    def chunk_step(chunk, carry):
        units_of(chunk, pairs)
        start_runs(chunk)
        return carry

    lax.fori_loop(0, last, chunk_step, 0)
    units_of(last, pairs)
    parts[last] = (total[...] * factor).astype(jnp.bfloat16).reshape(levels, ROWS, width)
    for step in (2, 1, 3, 0):
        run = (mem_x + step) % n_run
        start_last(run * 2 + 1 - mem_y)
        if step:
            start_last(run * 2 + mem_y)
    for chunk in range(last):
        finish(chunk)
    finish_last()

    wait_for(columns.at[:, :, pl.ds(0, levels - levels_own)], send_sem)
    wait_for(runs.at[:, pl.ds(0, n_run - 1)], run_send)
    if HALF:
        wait_for(halves, half_send)
    wait_for(arrived.at[pl.ds(0, n_mem - 1)], last_send)


def local(alpha, ens_pert, vert_sqrt, lat_sqrt):
    n_lon, n_mem = lax.axis_size("lon"), lax.axis_size("mem")
    members, levels_own, _, width = alpha.shape
    _, levels, own_rows, _ = ens_pert.shape
    chunks = own_rows // ROWS
    units = chunks * (members // PAIR)
    stacked = levels * ROWS
    levels_out = levels // n_mem
    factor = 1.0 / math.sqrt(members * n_mem)
    hbm = pl.BlockSpec(memory_space=pltpu.HBM)
    half, full = jnp.bfloat16, jnp.float32
    early = chunks - 1
    return pl.pallas_call(
        functools.partial(kernel, factor, n_lon, n_mem),
        out_shape=pltpu.VMEM((levels_out, own_rows, width), full),
        in_specs=[hbm] * 4,
        out_specs=pl.BlockSpec(memory_space=pltpu.VMEM),
        scratch_shapes=[
            pltpu.VMEM((chunks, members, levels, ROWS, width), half),
            pltpu.VMEM((chunks, members, levels, ROWS, width), half),
            pltpu.VMEM((PAIR, *alpha.shape[1:]), half),
            pltpu.VMEM((levels, levels), half),
            pltpu.VMEM((stacked, stacked), half),
            pltpu.VMEM((PAIR * width, PAIR * width), half),
            pltpu.VMEM((stacked, width), full),
            pltpu.VMEM((chunks, levels, ROWS, width), half),
            pltpu.VMEM((early, n_mem // 2, 2 * levels_out, ROWS, width), half),
            pltpu.VMEM((early, levels_out, ROWS, width), full),
            pltpu.VMEM((early, levels_out, ROWS, width), half),
            pltpu.VMEM((early, levels_out, ROWS, width), half),
            pltpu.VMEM((n_mem, levels_out, ROWS, width), half),
            pltpu.SemaphoreType.DMA,
            pltpu.SemaphoreType.DMA((1 + PAIR,)),
            pltpu.SemaphoreType.DMA((chunks,)),
            pltpu.SemaphoreType.DMA((chunks,)),
            pltpu.SemaphoreType.DMA,
            pltpu.SemaphoreType.DMA((units,)),
            pltpu.SemaphoreType.DMA,
            pltpu.SemaphoreType.DMA((early,)),
            pltpu.SemaphoreType.DMA,
            pltpu.SemaphoreType.DMA((early,)),
            pltpu.SemaphoreType.DMA,
            pltpu.SemaphoreType.DMA,
        ],
        compiler_params=pltpu.CompilerParams(
            collective_id=0, has_side_effects=True, vmem_limit_bytes=LIMIT * 2**20
        ),
    )(*(pltpu.with_memory_space_constraint(x, pltpu.HBM) for x in (alpha, ens_pert, vert_sqrt, lat_sqrt)))


def solution(mesh):
    placed = (P("mem", "lon", None, None), P("mem", None, "lon", None), P(), P())
    return jax.shard_map(
        local, mesh=mesh, in_specs=placed, out_specs=P("mem", "lon", None), check_vma=False
    )
```

time: 147 us -> 131 us (0.89)
  Pallas kernels: 144 us -> 130 us
    pallas_call x1, Pallas kernels: 144 us -> 130 us  [local(): pl.pallas_call(functools.partial(kernel, factor, n_lon, n_mem), out_shape...]
where the time goes in v2:
time: 131 us
  Pallas kernels  130 us (99%)
    pallas_call x1, Pallas kernels, local(): pl.pallas_call(functools.partial(kernel, factor, n_lon, n_mem), out_shape...  130 us

profile of v2, /device:TPU:1, one launch (start us, length us, event | category | flops | bytes accessed | tf_op | source)
XLA Modules:
  0.0 130.7 jit_solution(18057550724111903959)
XLA Ops:
  0.0 130.0 %shard_map.46 = f32[16,32,128]{2,1,0:T(8,128)S(1)} custom-call(bf16[10,8,512,128]{3,2,1,0:T(8,128)(2,1)} %alpha_ref.1, bf16[10,128,32,128]{3,2,1,0:T(8,128)(2,1)} %pert_ref.1, bf16[128,128]{1,0:T(8,128)(2,1)} %vert_ref.1, bf16[128,128]{1,0:T(8,128)(2,1)} %lat_ref.1), custom_call_target="tpu_custom_call" | custom-call | tf_op jit(solution)/shard_map/pallas_call | solution.py:285
  130.0 0.7 copy.6

commit v3 on v2

--- a/solution.py
+++ b/solution.py
@@ -11,10 +11,10 @@
 MESH = pl.DeviceIdType.MESH
 ROWS = 8
 PAIR = 2
-WINDOW = 15
+SEQ = 0
+SPLIT = 1
+ORDER = 4
 LIMIT = 54
-HALF = True
-STAGGER = True
 
 
 def kernel(
@@ -40,10 +40,15 @@
         y, z, c = lon // 8, (lon // 2) % 4, lon % 2
         return ((y + dy) % 2) * 8 + ((z + dz) % 4) * 2 + (c + dc) % 2
 
+    offsets = {
+        1: [(dy, dz) for dz in (2, 1, 3, 0) for dy in (1, 0)],
+        2: [(1, 2), (0, 1), (0, 3), (1, 0), (0, 2), (1, 1), (1, 3), (0, 0)],
+        3: [(0, 0), (1, 0), (0, 1), (0, 3), (1, 1), (1, 3), (0, 2), (1, 2)],
+        4: [(1, 2), (1, 1), (1, 3), (1, 0), (0, 2), (0, 1), (0, 3), (0, 0)],
+        5: [(0, 2), (0, 1), (0, 3), (1, 2), (1, 1), (1, 3), (1, 0), (0, 0)],
+    }[ORDER]
     lon_peers = [
-        lon_peer(dy, dz, dc)
-        for dz in (2, 1, 3, 0) for dy in (1, 0) for dc in (0, 1)
-        if (dy, dz, dc) != (0, 0, 0)
+        lon_peer(dy, dz, dc) for dy, dz in offsets for dc in (0, 1) if (dy, dz, dc) != (0, 0, 0)
     ]
     mem_peers = [(mem + step) % n_mem for step in range(1, n_mem)]
 
@@ -70,48 +75,30 @@
 
     def send_to(peer, source, unit):
         chunk, pair = unit // pairs, unit % pairs
-        group = pl.ds(pair * PAIR, PAIR)
         rows = pl.ds(pl.multiple_of(peer * own_rows + chunk * ROWS, ROWS), ROWS)
-        pltpu.make_async_remote_copy(
-            src_ref=source.at[group, :, rows, :],
-            dst_ref=columns.at[chunk, group, pl.ds(lon * levels_own, levels_own)],
-            send_sem=send_sem, recv_sem=recv_sem.at[unit],
-            device_id={"lon": peer, "mem": mem}, device_id_type=MESH,
-        ).start()
+        for k in range(SPLIT):
+            group = pl.ds(pair * PAIR + k * (PAIR // SPLIT), PAIR // SPLIT)
+            pltpu.make_async_remote_copy(
+                src_ref=source.at[group, :, rows, :],
+                dst_ref=columns.at[chunk, group, pl.ds(lon * levels_own, levels_own)],
+                send_sem=send_sem, recv_sem=recv_sem.at[unit],
+                device_id={"lon": peer, "mem": mem}, device_id_type=MESH,
+            ).start()
 
     def send(unit, carry):
         for peer in lon_peers:
             send_to(peer, alpha_ref, unit)
         return carry
 
-    def send_late(step):
-        core, pair = step // pairs, step % pairs
+    def send_late(core, pair):
         unit = last * pairs + pair
-        for dz in (2, 1, 3, 0):
-            for dy in (1, 0):
-                if (dy, dz) != (0, 0):
-                    send_to(lon_peer(dy, dz, core + lon), alpha_ref, unit)
+        for dy, dz in offsets:
+            if (dy, dz) != (0, 0):
+                send_to(lon_peer(dy, dz, core + lon), alpha_ref, unit)
 
         @pl.when(lon % 2 != core)
         def _():
             send_to(lon_peer(0, 0, 1), alpha_ref, unit)
-
-    def send_ahead(unit):
-        early = last * pairs
-        if not STAGGER:
-            @pl.when(unit < units)
-            def _():
-                send(unit, 0)
-            return
-
-        @pl.when(unit < early)
-        def _():
-            send(unit, 0)
-
-        @pl.when((unit >= early) & (unit < units))
-        def _():
-            for step in range(2):
-                send_late((unit - early) * 2 + step)
 
     stage = pltpu.make_async_copy(alpha_ref.at[pl.ds(0, PAIR)], staged, stage_sem)
     stage.start()
@@ -123,7 +110,14 @@
 
     for peer in lon_peers:
         send_to(peer, staged, 0)
-    lax.fori_loop(1, min(WINDOW, units), send, 0)
+    lax.fori_loop(1, last * pairs, send, 0)
+    orders = [
+        [(core, pair) for core in range(2) for pair in range(pairs)],
+        [(0, 0), (1, 0), (0, 1), (1, 1), (0, 2), (0, 3), (0, 4), (1, 2), (1, 3), (1, 4)],
+        [(0, 0), (1, 0), (0, 1), (0, 2), (0, 3), (0, 4), (1, 1), (1, 2), (1, 3), (1, 4)],
+    ]
+    for core, pair in orders[SEQ]:
+        send_late(core, pair)
     lat_copies = [
         pltpu.make_async_copy(
             lat_ref, lat_two.at[pl.ds(k * width, width), pl.ds(k * width, width)], small_sem.at[1 + k]
@@ -186,12 +180,10 @@
 
         halves[chunk] = summed(1 - mem_y).astype(jnp.bfloat16)
         held[chunk] = summed(mem_y)
-        if HALF:
-            to_device(halves.at[chunk], second.at[chunk], half_send, half_recv.at[chunk], mem_x * 2 + 1 - mem_y)
+        to_device(halves.at[chunk], second.at[chunk], half_send, half_recv.at[chunk], mem_x * 2 + 1 - mem_y)
 
     def finish(chunk):
-        if HALF:
-            wait_for(second.at[chunk], half_recv.at[chunk])
+        wait_for(second.at[chunk], half_recv.at[chunk])
         out_ref[:, pl.ds(chunk * ROWS, ROWS), :] = held[chunk] + second[chunk].astype(jnp.float32)
 
     def start_last(peer):
@@ -231,9 +223,6 @@
         total[...] = jnp.zeros_like(total)
 
         def unit_step(pair, carry):
-            unit = chunk * pairs + pair
-
-            send_ahead(unit + WINDOW)
 
             both = landed(chunk, pair)
 
@@ -253,21 +242,39 @@
 
     lax.fori_loop(0, last, chunk_step, 0)
     units_of(last, pairs)
-    parts[last] = (total[...] * factor).astype(jnp.bfloat16).reshape(levels, ROWS, width)
-    for step in (2, 1, 3, 0):
-        run = (mem_x + step) % n_run
-        start_last(run * 2 + 1 - mem_y)
-        if step:
-            start_last(run * 2 + mem_y)
-    for chunk in range(last):
-        finish(chunk)
-    finish_last()
+    own_core = lon % 2
+
+    @pl.when(own_core == 0)
+    def _():
+        start_runs(last)
+        start_half(last)
+        for chunk in range(chunks):
+            finish(chunk)
+
+    @pl.when(own_core == 1)
+    def _():
+        parts[last] = (total[...] * factor).astype(jnp.bfloat16).reshape(levels, ROWS, width)
+        for step in (2, 1, 3, 0):
+            run = (mem_x + step) % n_run
+            start_last(run * 2 + 1 - mem_y)
+            if step:
+                start_last(run * 2 + mem_y)
+        for chunk in range(last):
+            finish(chunk)
+        finish_last()
 
     wait_for(columns.at[:, :, pl.ds(0, levels - levels_own)], send_sem)
-    wait_for(runs.at[:, pl.ds(0, n_run - 1)], run_send)
-    if HALF:
-        wait_for(halves, half_send)
-    wait_for(arrived.at[pl.ds(0, n_mem - 1)], last_send)
+    wait_for(runs.at[pl.ds(0, last), pl.ds(0, n_run - 1)], run_send)
+    wait_for(halves.at[pl.ds(0, last)], half_send)
+
+    @pl.when(own_core == 0)
+    def _():
+        wait_for(runs.at[last, pl.ds(0, n_run - 1)], run_send)
+        wait_for(halves.at[last], half_send)
+
+    @pl.when(own_core == 1)
+    def _():
+        wait_for(arrived.at[pl.ds(0, n_mem - 1)], last_send)
 
 
 def local(alpha, ens_pert, vert_sqrt, lat_sqrt):
@@ -281,7 +288,6 @@
     factor = 1.0 / math.sqrt(members * n_mem)
     hbm = pl.BlockSpec(memory_space=pltpu.HBM)
     half, full = jnp.bfloat16, jnp.float32
-    early = chunks - 1
     return pl.pallas_call(
         functools.partial(kernel, factor, n_lon, n_mem),
         out_shape=pltpu.VMEM((levels_out, own_rows, width), full),
@@ -296,10 +302,10 @@
             pltpu.VMEM((PAIR * width, PAIR * width), half),
             pltpu.VMEM((stacked, width), full),
             pltpu.VMEM((chunks, levels, ROWS, width), half),
-            pltpu.VMEM((early, n_mem // 2, 2 * levels_out, ROWS, width), half),
-            pltpu.VMEM((early, levels_out, ROWS, width), full),
-            pltpu.VMEM((early, levels_out, ROWS, width), half),
-            pltpu.VMEM((early, levels_out, ROWS, width), half),
+            pltpu.VMEM((chunks, n_mem // 2, 2 * levels_out, ROWS, width), half),
+            pltpu.VMEM((chunks, levels_out, ROWS, width), full),
+            pltpu.VMEM((chunks, levels_out, ROWS, width), half),
+            pltpu.VMEM((chunks, levels_out, ROWS, width), half),
             pltpu.VMEM((n_mem, levels_out, ROWS, width), half),
             pltpu.SemaphoreType.DMA,
             pltpu.SemaphoreType.DMA((1 + PAIR,)),
@@ -308,9 +314,9 @@
             pltpu.SemaphoreType.DMA,
             pltpu.SemaphoreType.DMA((units,)),
             pltpu.SemaphoreType.DMA,
-            pltpu.SemaphoreType.DMA((early,)),
-            pltpu.SemaphoreType.DMA,
-            pltpu.SemaphoreType.DMA((early,)),
+            pltpu.SemaphoreType.DMA((chunks,)),
+            pltpu.SemaphoreType.DMA,
+            pltpu.SemaphoreType.DMA((chunks,)),
             pltpu.SemaphoreType.DMA,
             pltpu.SemaphoreType.DMA,
         ],

time: 131 us -> 130 us (level)
  no operation moved by 1% of the time
where the time goes in v3:
time: 130 us
  Pallas kernels  129 us (99%)
    pallas_call x1, Pallas kernels, local(): pl.pallas_call(functools.partial(kernel, factor, n_lon, n_mem), out_shape...  129 us

profile of v3, /device:TPU:1, one launch (start us, length us, event | category | flops | bytes accessed | tf_op | source)
XLA Modules:
  0.0 129.7 jit_solution(15002007984719024061)
XLA Ops:
  0.0 129.0 %shard_map.46 = f32[16,32,128]{2,1,0:T(8,128)S(1)} custom-call(bf16[10,8,512,128]{3,2,1,0:T(8,128)(2,1)} %alpha_ref.1, bf16[10,128,32,128]{3,2,1,0:T(8,128)(2,1)} %pert_ref.1, bf16[128,128]{1,0:T(8,128)(2,1)} %vert_ref.1, bf16[128,128]{1,0:T(8,128)(2,1)} %lat_ref.1), custom_call_target="tpu_custom_call" | custom-call | tf_op jit(solution)/shard_map/pallas_call | solution.py:291
  129.0 0.7 copy.6

commit v4 on v3

--- a/solution.py
+++ b/solution.py
@@ -11,9 +11,7 @@
 MESH = pl.DeviceIdType.MESH
 ROWS = 8
 PAIR = 2
-SEQ = 0
-SPLIT = 1
-ORDER = 4
+HEAD = 2
 LIMIT = 54
 
 
@@ -21,7 +19,7 @@
     factor, n_lon, n_mem, alpha_ref, pert_ref, vert_ref, lat_ref, out_ref,
     columns, perts, staged, vert, kron, lat_two, total, parts, runs, held, halves, second, arrived,
     stage_sem, small_sem, own_sem, pert_sem, send_sem, recv_sem,
-    run_send, run_recv, half_send, half_recv, last_send, last_recv,
+    here_sem, run_send, run_recv, half_send, half_recv, last_send, last_recv,
 ):
     lon, mem = lax.axis_index("lon"), lax.axis_index("mem")
     members, levels_own = alpha_ref.shape[0], alpha_ref.shape[1]
@@ -40,26 +38,26 @@
         y, z, c = lon // 8, (lon // 2) % 4, lon % 2
         return ((y + dy) % 2) * 8 + ((z + dz) % 4) * 2 + (c + dc) % 2
 
-    offsets = {
-        1: [(dy, dz) for dz in (2, 1, 3, 0) for dy in (1, 0)],
-        2: [(1, 2), (0, 1), (0, 3), (1, 0), (0, 2), (1, 1), (1, 3), (0, 0)],
-        3: [(0, 0), (1, 0), (0, 1), (0, 3), (1, 1), (1, 3), (0, 2), (1, 2)],
-        4: [(1, 2), (1, 1), (1, 3), (1, 0), (0, 2), (0, 1), (0, 3), (0, 0)],
-        5: [(0, 2), (0, 1), (0, 3), (1, 2), (1, 1), (1, 3), (1, 0), (0, 0)],
-    }[ORDER]
-    lon_peers = [
-        lon_peer(dy, dz, dc) for dy, dz in offsets for dc in (0, 1) if (dy, dz, dc) != (0, 0, 0)
-    ]
+    near = [(1, 0, 0), (1, 0, 1), *((0, dz, dc) for dz in (2, 1, 3) for dc in (0, 1)), (0, 0, 1)]
+    far = [(1, dz, dc) for dz in (2, 1, 3) for dc in (0, 1)]
+    lon_near = [lon_peer(*offset) for offset in near]
+    lon_far = [lon_peer(*offset) for offset in far]
+    lon_peers = lon_far + lon_near
     mem_peers = [(mem + step) % n_mem for step in range(1, n_mem)]
 
     def wait_for(ref, sem):
         pltpu.make_async_copy(ref, ref, sem).wait()
 
+    mem_near = [(mem_x + step) % n_run * 2 + mem_y for step in range(1, n_run)] + [mem_x * 2 + 1 - mem_y]
     barrier = pltpu.get_barrier_semaphore()
-    for peer in lon_peers:
-        pl.semaphore_signal(barrier, inc=1, device_id={"lon": peer, "mem": mem}, device_id_type=MESH)
-    for peer in mem_peers:
-        pl.semaphore_signal(barrier, inc=1, device_id={"lon": lon, "mem": peer}, device_id_type=MESH)
+
+    def say(sem, lon_to, mem_to):
+        pl.semaphore_signal(sem, inc=1, device_id={"lon": lon_to, "mem": mem_to}, device_id_type=MESH)
+
+    for peer in lon_near:
+        say(barrier, peer, mem)
+    for peer in mem_near:
+        say(barrier, lon, peer)
 
     def own_copy(chunk):
         rows = pl.ds(pl.multiple_of(lon * own_rows + chunk * ROWS, ROWS), ROWS)
@@ -74,31 +72,30 @@
         return pltpu.make_async_copy(pert_ref.at[:, :, rows, :], perts.at[chunk], pert_sem.at[chunk])
 
     def send_to(peer, source, unit):
-        chunk, pair = unit // pairs, unit % pairs
+        chunk, group = unit // pairs, pl.ds(unit % pairs * PAIR, PAIR)
         rows = pl.ds(pl.multiple_of(peer * own_rows + chunk * ROWS, ROWS), ROWS)
-        for k in range(SPLIT):
-            group = pl.ds(pair * PAIR + k * (PAIR // SPLIT), PAIR // SPLIT)
-            pltpu.make_async_remote_copy(
-                src_ref=source.at[group, :, rows, :],
-                dst_ref=columns.at[chunk, group, pl.ds(lon * levels_own, levels_own)],
-                send_sem=send_sem, recv_sem=recv_sem.at[unit],
-                device_id={"lon": peer, "mem": mem}, device_id_type=MESH,
-            ).start()
+        pltpu.make_async_remote_copy(
+            src_ref=source.at[group, :, rows, :],
+            dst_ref=columns.at[chunk, group, pl.ds(lon * levels_own, levels_own)],
+            send_sem=send_sem, recv_sem=recv_sem.at[unit],
+            device_id={"lon": peer, "mem": mem}, device_id_type=MESH,
+        ).start()
+
+    def send_unit(unit, peers, source=alpha_ref):
+        for peer in peers:
+            send_to(peer, source, unit)
 
     def send(unit, carry):
-        for peer in lon_peers:
-            send_to(peer, alpha_ref, unit)
+        send_unit(unit, lon_peers)
         return carry
 
-    def send_late(core, pair):
-        unit = last * pairs + pair
-        for dy, dz in offsets:
-            if (dy, dz) != (0, 0):
-                send_to(lon_peer(dy, dz, core + lon), alpha_ref, unit)
+    def send_late(core, unit):
+        offsets = [(1, 2), (1, 1), (1, 3), (1, 0), (0, 2), (0, 1), (0, 3)]
+        send_unit(unit, [lon_peer(dy, dz, core + lon) for dy, dz in offsets])
 
         @pl.when(lon % 2 != core)
         def _():
-            send_to(lon_peer(0, 0, 1), alpha_ref, unit)
+            send_unit(unit, [lon_peer(0, 0, 1)])
 
     stage = pltpu.make_async_copy(alpha_ref.at[pl.ds(0, PAIR)], staged, stage_sem)
     stage.start()
@@ -106,18 +103,21 @@
     vert_copy.start()
     lat_two[...] = jnp.zeros_like(lat_two)
     stage.wait()
-    pl.semaphore_wait(barrier, len(lon_peers) + len(mem_peers))
-
-    for peer in lon_peers:
-        send_to(peer, staged, 0)
-    lax.fori_loop(1, last * pairs, send, 0)
-    orders = [
-        [(core, pair) for core in range(2) for pair in range(pairs)],
-        [(0, 0), (1, 0), (0, 1), (1, 1), (0, 2), (0, 3), (0, 4), (1, 2), (1, 3), (1, 4)],
-        [(0, 0), (1, 0), (0, 1), (0, 2), (0, 3), (0, 4), (1, 1), (1, 2), (1, 3), (1, 4)],
-    ]
-    for core, pair in orders[SEQ]:
-        send_late(core, pair)
+    def head(unit, peers):
+        send_unit(unit, peers, staged if unit == 0 else alpha_ref)
+
+    pl.semaphore_wait(barrier, len(lon_near) + len(mem_near))
+    say(here_sem, lon_peer(1, 0, 0), mem)
+    say(here_sem, lon, mem_x * 2 + 1 - mem_y)
+    for unit in range(HEAD):
+        head(unit, lon_near)
+    pl.semaphore_wait(here_sem, 2)
+    for unit in range(HEAD):
+        head(unit, lon_far)
+    lax.fori_loop(HEAD, last * pairs, send, 0)
+    for core in range(2):
+        for pair in range(pairs):
+            send_late(core, last * pairs + pair)
     lat_copies = [
         pltpu.make_async_copy(
             lat_ref, lat_two.at[pl.ds(k * width, width), pl.ds(k * width, width)], small_sem.at[1 + k]
@@ -158,8 +158,10 @@
             device_id={"lon": lon, "mem": peer}, device_id_type=MESH,
         ).start()
 
+    def keep(chunk, value):
+        parts[chunk] = (value * factor).astype(jnp.bfloat16).reshape(levels, ROWS, width)
+
     def start_runs(chunk):
-        parts[chunk] = (total[...] * factor).astype(jnp.bfloat16).reshape(levels, ROWS, width)
         for step in (2, 1, 3):
             peer = (mem_x + step) % n_run
             to_device(
@@ -198,22 +200,16 @@
             value = value + arrived[source].astype(jnp.float32)
         out_ref[:, pl.ds(last * ROWS, ROWS), :] = value
 
-    def landed(chunk, pair):
+    def added(value, chunk, pair):
+        first = pair * PAIR
         wait_for(
-            columns.at[chunk, pl.ds(pair * PAIR, PAIR), pl.ds(0, levels - levels_own)],
-            recv_sem.at[chunk * pairs + pair],
+            columns.at[chunk, pl.ds(first, PAIR), pl.ds(0, levels - levels_own)], recv_sem.at[chunk * pairs + pair]
         )
-        return jnp.concatenate(
-            [columns[chunk, pair * PAIR + k].reshape(stacked, width) for k in range(PAIR)], axis=1
-        )
-
-    def added(value, chunk, pair, both, first_level, n_levels):
-        rows = pl.ds(first_level * ROWS, n_levels * ROWS)
-        vertical = jnp.dot(kron[rows, :], both, preferred_element_type=jnp.float32).astype(jnp.bfloat16)
+        fields = jnp.concatenate([columns[chunk, first + k].reshape(stacked, width) for k in range(PAIR)], axis=1)
+        vertical = jnp.dot(kron[...], fields, preferred_element_type=jnp.float32).astype(jnp.bfloat16)
         localized = jnp.dot(vertical, lat_two[...], preferred_element_type=jnp.float32)
         for k in range(PAIR):
-            pert = perts[chunk, pair * PAIR + k, pl.ds(first_level, n_levels)]
-            pert = pert.reshape(n_levels * ROWS, width).astype(jnp.float32)
+            pert = perts[chunk, first + k].reshape(stacked, width).astype(jnp.float32)
             value = value + pert * localized[:, k * width : (k + 1) * width]
         return value
 
@@ -224,24 +220,25 @@
 
         def unit_step(pair, carry):
 
-            both = landed(chunk, pair)
+            total[...] = added(total[...], chunk, pair)
 
             @pl.when((chunk > 0) & (pair == jnp.where(chunk < last, 1, 1 - lon % 2)))
             def _():
                 start_half(chunk - 1)
 
-            total[...] = added(total[...], chunk, pair, both, 0, levels)
             return carry
 
         lax.fori_loop(0, n_pairs, unit_step, 0)
 
     def chunk_step(chunk, carry):
         units_of(chunk, pairs)
+        keep(chunk, total[...])
         start_runs(chunk)
         return carry
 
     lax.fori_loop(0, last, chunk_step, 0)
     units_of(last, pairs)
+    keep(last, total[...])
     own_core = lon % 2
 
     @pl.when(own_core == 0)
@@ -253,7 +250,6 @@
 
     @pl.when(own_core == 1)
     def _():
-        parts[last] = (total[...] * factor).astype(jnp.bfloat16).reshape(levels, ROWS, width)
         for step in (2, 1, 3, 0):
             run = (mem_x + step) % n_run
             start_last(run * 2 + 1 - mem_y)
@@ -313,6 +309,7 @@
             pltpu.SemaphoreType.DMA((chunks,)),
             pltpu.SemaphoreType.DMA,
             pltpu.SemaphoreType.DMA((units,)),
+            pltpu.SemaphoreType.REGULAR,
             pltpu.SemaphoreType.DMA,
             pltpu.SemaphoreType.DMA((chunks,)),
             pltpu.SemaphoreType.DMA,

time: 130 us -> 129 us (level)
  no operation moved by 1% of the time
where the time goes in v4:
time: 129 us
  Pallas kernels  128 us (99%)
    pallas_call x1, Pallas kernels, local(): pl.pallas_call(functools.partial(kernel, factor, n_lon, n_mem), out_shape...  128 us

profile of v4, /device:TPU:1, one launch (start us, length us, event | category | flops | bytes accessed | tf_op | source)
XLA Modules:
  0.0 129.0 jit_solution(4174273350688643747)
XLA Ops:
  0.0 128.2 %shard_map.46 = f32[16,32,128]{2,1,0:T(8,128)S(1)} custom-call(bf16[10,8,512,128]{3,2,1,0:T(8,128)(2,1)} %alpha_ref.1, bf16[10,128,32,128]{3,2,1,0:T(8,128)(2,1)} %pert_ref.1, bf16[128,128]{1,0:T(8,128)(2,1)} %vert_ref.1, bf16[128,128]{1,0:T(8,128)(2,1)} %lat_ref.1), custom_call_target="tpu_custom_call" | custom-call | tf_op jit(solution)/shard_map/pallas_call | solution.py:287
  128.3 0.7 copy.6
